TPU v7x, 512 devices: a whole 4x8x8 slice. The times are simulated.
512 devices in a mesh: gx: 8 (over z_lo, core), gy: 8 (over y), gz: 8 (over x, z_hi).
Axes of the slice: x: 4, y: 8, z: 8 (z_hi: 2, z_lo: 4; z = z_hi * 4 + z_lo), core: 2. Of those that a mesh axis runs over, the one named last changes fastest.
Arguments:
- head_inputs: bfloat16 [131072, 2048], P(('gx', 'gy', 'gz')), may hold values from -6 to 6
- step_raw: float32 [131072, 32], P(('gx', 'gy', 'gz')), may hold values from -4 to 4
- state_in: bfloat16 [131072, 128], P(('gx', 'gy', 'gz')), may hold values from -0.119628906 to 0.119628906
- state_out: bfloat16 [131072, 128], P(('gx', 'gy', 'gz')), may hold values from -0.119628906 to 0.119628906
- decay_log: float32 [32], replicated, may hold values from -13.5 to -3
- step_bias: float32 [32], replicated, may hold values from -1 to 0.5
- skip_gain: float32 [32], replicated, may hold values from 0.5 to 1.5
- checkpoints: bfloat16 [512, 32, 64, 128], P(('gx', 'gy'), None, 'gz'), may hold values from -6 to 6
- out_grad: bfloat16 [131072, 2048], P(('gx', 'gy', 'gz')), may hold values from -6 to 6
Outputs:
- input_grad: bfloat16 [131072, 2048], P(('gx', 'gy', 'gz'))
- step_grad: float32 [131072, 32], P(('gx', 'gy', 'gz'))
- state_in_grad: float32 [131072, 128], P(('gx', 'gy', 'gz'))
- state_out_grad: float32 [131072, 128], P(('gx', 'gy', 'gz'))
- decay_log_grad: float32 [32], replicated
- step_bias_grad: float32 [32], replicated
- skip_gain_grad: float32 [32], replicated
All inputs are finite; a program needn't handle non-finite values.
Results may differ from a plain program's by a relative error of at most 0.00065.
Values may be sent and summed in bfloat16 or wider, within the bound.
A program may use at most 128 MiB of HBM per device.

v0:
```python
import jax
import jax.numpy as jnp
from jax import lax
from jax.sharding import Mesh
from jax.sharding import PartitionSpec as P

GZ = ("gz_0", "gz_1")
GX_GY = ("gx_0", "gx_1", "gy")
GX_GY_GZ = ("gx_0", "gx_1", "gy", "gz_0", "gz_1")
highest = lax.Precision.HIGHEST


def neutral_like(array, identity):
    return jax.tree.map(
        lambda a, e: jnp.broadcast_to(jnp.asarray(e, a.dtype), a.shape), array, identity
    )


def carried_in(array, axes, combine, identity):
    before = start = neutral_like(array, identity)
    so_far = array
    for axis in reversed(axes):
        length, index = (lax.axis_size(axis), lax.axis_index(axis))
        pieces = jax.tree.map(lambda part: lax.all_gather(part, axis), so_far)
        inside, so_far = (start, start)
        for k in reversed(range(length)):
            passed = k > index
            so_far = combine(so_far, jax.tree.map(lambda part: part[k], pieces))
            inside = jax.tree.map(lambda new, old: jnp.where(passed, new, old), so_far, inside)
        before = combine(inside, before)
    return before


def by_axis(array, axes):
    for axis in axes:
        array = lax.psum(array, axis)
    return array


def block_forward(inputs, raw, b_mat, scores, read, decay_log, bias, skip, start):
    step = jax.nn.softplus(raw + bias)
    cum = jnp.cumsum(step * -jnp.exp(decay_log), axis=0)
    length = inputs.shape[0]
    rows = lax.broadcasted_iota(jnp.int32, (length, length), 0)
    cols = lax.broadcasted_iota(jnp.int32, (length, length), 1)
    lower = rows >= cols
    ctrans = cum.T
    gap = ctrans[:, :, None] - ctrans[:, None, :]
    mix = jnp.where(lower, jnp.exp(jnp.where(lower, gap, 0.0)), 0.0) * scores * step.T[:, None, :]
    inner = jnp.einsum("hts,shp->thp", mix, inputs, precision=highest)
    carried = read * jnp.exp(cum)[:, :, None]
    result = inner + carried + skip[None, :, None] * inputs
    tail = jnp.exp(cum[-1][None, :] - cum) * step
    final = jnp.exp(cum[-1])[:, None, None] * start + jnp.einsum(
        "sh,shp,sn->hpn", tail, inputs, b_mat, precision=highest
    )
    return (result, final)


def span_forward(inputs, raw, b_mat, scores, read, decay_log, bias, skip, start):
    length, heads = raw.shape
    width = inputs.shape[1] // heads
    states = start.shape[2]
    block = min(8, heads)
    blocks = heads // block
    grouped = inputs.reshape(length, blocks, block, width).transpose(1, 0, 2, 3)
    read_g = read.reshape(length, blocks, block, width).transpose(1, 0, 2, 3)
    raw_g = raw.reshape(length, blocks, block).transpose(1, 0, 2)

    def one_block(items):
        return block_forward(
            items[0], items[1], b_mat, scores, items[2], items[3], items[4], items[5], items[6]
        )

    result, final = lax.map(
        one_block,
        (
            grouped,
            raw_g,
            read_g,
            decay_log.reshape(blocks, block),
            bias.reshape(blocks, block),
            skip.reshape(blocks, block),
            start.reshape(blocks, block, width, states),
        ),
    )
    result = result.transpose(1, 0, 2, 3).reshape(length, heads * width)
    return (result, final.reshape(heads, width, states))


def combine(earlier, later):
    return (earlier[0] * later[0], later[0][:, None, None] * earlier[1] + later[1])


def local(
    head_inputs,
    step_raw,
    state_in,
    state_out,
    decay_log,
    step_bias,
    skip_gain,
    checkpoints,
    out_grad,
):
    entering = lax.all_to_all(checkpoints, GZ, split_axis=0, concat_axis=2, tiled=True)[0]
    start = entering.astype(jnp.float32)
    length, heads = step_raw.shape
    width = head_inputs.shape[1] // heads
    states = state_in.shape[1]
    c_mat = state_out.astype(jnp.float32)
    b_mat = state_in.astype(jnp.float32)
    grad_rows = out_grad.astype(jnp.float32)
    step = jax.nn.softplus(step_raw + step_bias)
    cum = jnp.cumsum(step * -jnp.exp(decay_log), axis=0)
    weighted = (grad_rows.reshape(length, heads, width) * jnp.exp(cum)[:, :, None]).reshape(
        length, heads * width
    )
    local_term = jnp.dot(weighted.T, c_mat, precision=highest).reshape(heads, width, states)
    decays = jnp.exp(cum[-1])
    group = lax.axis_size(GZ)
    spread = jnp.broadcast_to(decays[None, :, None], (1, heads, group))
    got_decay, got_term = (
        lax.all_to_all(spread, GZ, split_axis=2, concat_axis=0, tiled=True),
        lax.all_to_all(local_term[None], GZ, split_axis=2, concat_axis=0, tiled=True),
    )
    got_decay = got_decay[:, :, 0]
    slice_width = got_term.shape[2]
    suffix_b = jnp.zeros((heads, slice_width, states), jnp.float32)
    suffix_a = jnp.ones((heads,), jnp.float32)
    inners = [None] * group
    leads = [None] * group
    for member in reversed(range(group)):
        inners[member] = suffix_b
        leads[member] = suffix_a
        suffix_b = got_term[member] + got_decay[member][:, None, None] * suffix_b
        suffix_a = got_decay[member] * suffix_a
    total = (suffix_a, suffix_b)
    neutral = (
        jnp.ones((heads,), jnp.float32),
        jnp.zeros((heads, slice_width, states), jnp.float32),
    )
    outer = carried_in(total, GX_GY, combine, neutral)
    carries = jnp.stack(
        [inners[member] + leads[member][:, None, None] * outer[1] for member in range(group)]
    )
    later = lax.all_to_all(carries, GZ, split_axis=0, concat_axis=2, tiled=True)[0]
    flat_start = entering.reshape(heads * width, states)
    scores = jnp.dot(state_out, state_in.T, preferred_element_type=jnp.float32)
    read = jnp.dot(state_out, flat_start.T, preferred_element_type=jnp.float32)
    _, pull = jax.vjp(
        span_forward,
        head_inputs.astype(jnp.float32),
        step_raw,
        b_mat,
        scores,
        read,
        decay_log,
        step_bias,
        skip_gain,
        start,
    )
    grads = pull((grad_rows, later))
    b_grad = grads[2] + jnp.dot(grads[3].T, c_mat, precision=highest)
    c_grad = jnp.dot(grads[3], b_mat, precision=highest) + jnp.dot(
        grads[4], flat_start.astype(jnp.float32), precision=highest
    )
    decay_sum, bias_sum, skip_sum = (
        by_axis(grads[5], GX_GY_GZ),
        by_axis(grads[6], GX_GY_GZ),
        by_axis(grads[7], GX_GY_GZ),
    )
    return (grads[0].astype(jnp.bfloat16), grads[1], b_grad, c_grad, decay_sum, bias_sum, skip_sum)


def solution(mesh):
    torus = Mesh(
        mesh.devices.reshape(4, 2, mesh.shape["gy"], 4, 2), ("gx_0", "gx_1", "gy", "gz_0", "gz_1")
    )
    return jax.shard_map(
        local,
        mesh=torus,
        in_specs=(
            P(GX_GY_GZ, None),
            P(GX_GY_GZ, None),
            P(GX_GY_GZ, None),
            P(GX_GY_GZ, None),
            P(),
            P(),
            P(),
            P(GX_GY, None, GZ, None),
            P(GX_GY_GZ, None),
        ),
        out_specs=(
            P(GX_GY_GZ, None),
            P(GX_GY_GZ, None),
            P(GX_GY_GZ, None),
            P(GX_GY_GZ, None),
            P(),
            P(),
            P(),
        ),
        check_vma=False,
    )
```

profile of v0, /device:TPU:64, one launch (start us, length us, event | category | flops | bytes accessed | tf_op | source)
XLA Modules:
  0.0 441.4 jit_solution(9832343445623595339)
XLA Ops:
  10.4 11.8 %all-to-all-start.1 = ((f32[1,32,8]{1,0,2:T(1,128)}), f32[1,32,8]{1,0,2:T(1,128)S(1)}, u32[]{:S(2)}, u32[]{:S(2)}) async-start(f32[1,32,8]{1,0,2:T(1,128)} %broadcast_in_dim.210), calls=%async_computation.1 | async-start | bytes 8192 | tf_op jit(solution)/shard_map/all_to_all | solution.py:124
  22.4 1.5 copy.168
  25.1 1.6 copy.171
  26.7 5.6 %all-to-all-done.1 = f32[1,32,8]{1,0,2:T(1,128)S(1)} async-done(((f32[1,32,8]{1,0,2:T(1,128)}), f32[1,32,8]{1,0,2:T(1,128)S(1)}, u32[]{:S(2)}, u32[]{:S(2)}) %all-to-all-start.1) | async-done | bytes 1056 | tf_op jit(solution)/shard_map/all_to_all | solution.py:124
  32.3 4.0 all-to-all-start
  37.5 29.1 %all-to-all-done = f32[1,32,64,128]{3,1,0,2:T(8,128)S(1)} async-done(((f32[1,32,64,128]{3,1,0,2:T(8,128)}), f32[1,32,64,128]{3,1,0,2:T(8,128)S(1)}, u32[]{:S(2)}, u32[]{:S(2)}) %all-to-all-start) | async-done | bytes 1048608 | tf_op jit(solution)/shard_map/all_to_all | solution.py:125
  68.3 4.2 all-to-all-start.3
  73.4 2.6 copy.164
  76.8 16.8 %all-gather = f32[8,1,32,1]{2,3,1,0:T(1,128)S(1)} all-gather(f32[1,1,32,1]{2,3,1,0:T(1,128)S(1)} %get-tuple-element.1868), channel_id=2, replica_groups=mesh['gx_0'=4,'gx_1'=2,'gy'=8,'gz_0'=4,'gz_1'=2] {'gy'}, dimensions={0}, use_global_device_ids=true | all-gather | bytes 1152 | tf_op jit(solution)/shard_map/all_gather | solution.py:24
  93.6 1.8 all-gather.1
  95.4 8.2 %all-gather.2 = f32[4,1,32]{2,1,0:T(1,128)S(1)} all-gather(f32[1,1,32]{2,1,0:T(1,128)S(1)} %get-tuple-element.1888), channel_id=1, replica_groups=mesh['gx_0'=4,'gx_1'=2,'gy'=8,'gz_0'=4,'gz_1'=2] {'gx_0'}, dimensions={0}, use_global_device_ids=true | all-gather | bytes 640 | tf_op jit(solution)/shard_map/all_gather | solution.py:24
  105.9 1.7 slice_add_fusion.6
  107.7 2.1 all_gather.28
  110.0 16.5 %all_gather.29 = f32[4,32,8,128]{3,2,1,0:T(8,128)S(1)} all-gather(f32[1,32,8,128]{3,2,1,0:T(8,128)S(1)} %slice_add_fusion.4), channel_id=1, replica_groups=mesh['gx_0'=4,'gx_1'=2,'gy'=8,'gz_0'=4,'gz_1'=2] {'gx_0'}, dimensions={0}, use_global_device_ids=true | all-gather | bytes 655360 | tf_op jit(solution)/shard_map/all_gather | solution.py:24
  126.6 2.2 add_dynamic-update-slice_fusion.6
  134.1 6.5 %all-to-all-start.2 = ((f32[8,32,8,128]{3,2,1,0:T(8,128)}), f32[8,32,8,128]{3,2,1,0:T(8,128)}, u32[]{:S(2)}, u32[]{:S(2)}) async-start(f32[8,32,8,128]{3,2,1,0:T(8,128)} %constant_dynamic-update-slice_fusion.3), calls=%async_computation.2 | async-start | bytes 2097152 | tf_op jit(solution)/shard_map/all_to_all | solution.py:147
  140.6 1.5 broadcast.740.clone.1
  145.8 57.4 %while.75 = (s32[]{:T(128)}, f32[4,256,8]{1,2,0:T(8,128)}, f32[4,8]{1,0:T(4,128)}, f32[4,1,8]{2,1,0:T(1,128)}, f32[4,256,8]{1,2,0:T(8,128)}, /*index=5*/f32[4,8,...) while((s32[]{:T(128)}, f32[4,256,8]{1,2,0:T(8,128)}, ...), condition=%wide.region_5.6_spmd.clone.clone, body=%wide.region_2.5_spmd.clone.clone.sunk | while | flops 3090474 | bytes 14180141 | solution.py:75
  147.4 4.2 multiply_dynamic-update-slice_fusion.4
  161.8 4.0 multiply_dynamic-update-slice_fusion.4
  176.1 4.2 multiply_dynamic-update-slice_fusion.4
  190.5 4.0 multiply_dynamic-update-slice_fusion.4
  208.8 1.8 convolution_bitcast_fusion.2
  210.5 2.3 copy.181
  212.9 1.6 broadcast.740
  216.8 157.2 %while.76 = (s32[]{:T(128)}, f32[256,256]{1,0:T(8,128)S(1)}, f32[256,128]{1,0:T(8,128)}, bf16[4,256,8,64]{1,3,2,0:T(8,128)(2,1)}, f32[4,256,8]{1,2,0:T(8,128)}, ...) while((s32[]{:T(128)}, f32[256,256]{1,0:T(8,128)S(1)}, ...), condition=%wide.region_19.20_spmd.clone.clone, body=%wide.region_6.19_spmd.clone.clone.sunk | while | flops 1215725568 | bytes 18326480 | solution.py:75
  217.4 2.5 fusion.152
  222.0 6.5 %fusion.150 = (f32[8,256]{1,0:T(8,128)}, f32[8,256]{1,0:T(8,128)}, f32[256,256]{1,0:T(8,128)S(1)}, f32[8,256]{1,0:T(8,128)}) fusion(f32[4,8,256,256]{3,2,1,0:T(8,128)} %get-tuple-element.2474, s32[]{:T(128)S(6)} %sub.146, f32[256,256]{1,0:T(8,128)S(1)} %bitcast.579, f32[8,256]{1,0:T(8,128)S(1)} %dynamic-slice_bitcast_fusion.6, ...), kind=kOutput, calls=%fused_computation.87.clone.1 | convolution fusion | flops 408348672 | bytes 7964160 | tf_op jit(solution)/shard_map/transpose(jvp())/while/body/eval_jaxpr/hts,shp->thp/dot_general | solution.py:50
  228.5 1.7 fusion.157
  232.3 1.4 fusion.159
  233.7 3.2 reduce-window.62
  240.1 1.4 fusion.160
  246.7 3.7 fusion.154
  253.3 2.8 fusion.151
  256.6 2.5 fusion.152
  261.3 6.5 %fusion.150 = (f32[8,256]{1,0:T(8,128)}, f32[8,256]{1,0:T(8,128)}, f32[256,256]{1,0:T(8,128)S(1)}, f32[8,256]{1,0:T(8,128)}) fusion(f32[4,8,256,256]{3,2,1,0:T(8,128)} %get-tuple-element.2474, s32[]{:T(128)S(6)} %sub.146, f32[256,256]{1,0:T(8,128)S(1)} %bitcast.579, f32[8,256]{1,0:T(8,128)S(1)} %dynamic-slice_bitcast_fusion.6, ...), kind=kOutput, calls=%fused_computation.87.clone.1 | convolution fusion | flops 408348672 | bytes 7964160 | tf_op jit(solution)/shard_map/transpose(jvp())/while/body/eval_jaxpr/hts,shp->thp/dot_general | solution.py:50
  267.8 1.7 fusion.157
  273.0 3.2 reduce-window.62
  279.3 1.4 fusion.160
  286.0 3.7 fusion.154
  292.5 2.8 fusion.151
  295.9 2.5 fusion.152
  300.6 6.5 %fusion.150 = (f32[8,256]{1,0:T(8,128)}, f32[8,256]{1,0:T(8,128)}, f32[256,256]{1,0:T(8,128)S(1)}, f32[8,256]{1,0:T(8,128)}) fusion(f32[4,8,256,256]{3,2,1,0:T(8,128)} %get-tuple-element.2474, s32[]{:T(128)S(6)} %sub.146, f32[256,256]{1,0:T(8,128)S(1)} %bitcast.579, f32[8,256]{1,0:T(8,128)S(1)} %dynamic-slice_bitcast_fusion.6, ...), kind=kOutput, calls=%fused_computation.87.clone.1 | convolution fusion | flops 408348672 | bytes 7964160 | tf_op jit(solution)/shard_map/transpose(jvp())/while/body/eval_jaxpr/hts,shp->thp/dot_general | solution.py:50
  307.1 1.7 fusion.157
  312.3 3.2 reduce-window.62
  318.6 1.4 fusion.160
  325.3 3.7 fusion.154
  331.9 2.8 fusion.151
  335.2 2.5 fusion.152
  339.9 6.5 %fusion.150 = (f32[8,256]{1,0:T(8,128)}, f32[8,256]{1,0:T(8,128)}, f32[256,256]{1,0:T(8,128)S(1)}, f32[8,256]{1,0:T(8,128)}) fusion(f32[4,8,256,256]{3,2,1,0:T(8,128)} %get-tuple-element.2474, s32[]{:T(128)S(6)} %sub.146, f32[256,256]{1,0:T(8,128)S(1)} %bitcast.579, f32[8,256]{1,0:T(8,128)S(1)} %dynamic-slice_bitcast_fusion.6, ...), kind=kOutput, calls=%fused_computation.87.clone.1 | convolution fusion | flops 408348672 | bytes 7964160 | tf_op jit(solution)/shard_map/transpose(jvp())/while/body/eval_jaxpr/hts,shp->thp/dot_general | solution.py:50
  346.4 1.7 fusion.157
  350.1 1.4 fusion.159
  351.6 3.2 reduce-window.62
  358.0 1.4 fusion.160
  364.6 3.7 fusion.154
  371.2 2.8 fusion.151
  377.5 1.9 convolution_add_fusion.1
  379.5 2.3 copy.184
  381.7 11.6 %all-reduce.4 = (f32[32]{0:T(128)S(1)}, f32[32]{0:T(128)S(1)}, f32[32]{0:T(128)S(1)}) all-reduce(f32[32]{0:T(128)S(1)} %reshape.895, f32[32]{0:T(128)S(1)} %reshape.896, f32[32]{0:T(128)S(1)} %reshape.897), channel_id=1, replica_groups=mesh['gx_0'=4,'gx_1'=2,'gy'=8,'gz_0'=4,'gz_1'=2] {'gx_0'}, use_global_device_ids=true, to_apply=%region_20.21 | all-reduce | flops 96 | bytes 768 | tf_op jit(solution)/shard_map/psum | solution.py:36
  393.3 2.5 all-reduce.6
  395.8 16.1 %all-reduce.2 = (f32[32]{0:T(128)S(1)}, f32[32]{0:T(128)S(1)}, f32[32]{0:T(128)S(1)}) all-reduce(f32[32]{0:T(128)S(1)} %get-tuple-element.1825, f32[32]{0:T(128)S(1)} %get-tuple-element.1826, f32[32]{0:T(128)S(1)} %get-tuple-element.1827), channel_id=1, replica_groups=mesh['gx_0'=4,'gx_1'=2,'gy'=8,'gz_0'=4,'gz_1'=2] {'gy'}, use_global_device_ids=true, to_apply=%region_22.23 | all-reduce | flops 96 | bytes 768 | tf_op jit(solution)/shard_map/psum | solution.py:36
  411.8 10.9 %all-reduce.3 = (f32[32]{0:T(128)S(1)}, f32[32]{0:T(128)S(1)}, f32[32]{0:T(128)S(1)}) all-reduce(f32[32]{0:T(128)S(1)} %get-tuple-element.1813, f32[32]{0:T(128)S(1)} %get-tuple-element.1814, f32[32]{0:T(128)S(1)} %get-tuple-element.1815), channel_id=1, replica_groups=mesh['gx_0'=4,'gx_1'=2,'gy'=8,'gz_0'=4,'gz_1'=2] {'gz_0'}, use_global_device_ids=true, to_apply=%region_23.24 | all-reduce | flops 96 | bytes 768 | tf_op jit(solution)/shard_map/psum | solution.py:36
  422.8 9.3 %all-reduce.5 = (f32[32]{0:T(128)}, f32[32]{0:T(128)}, f32[32]{0:T(128)}) all-reduce(f32[32]{0:T(128)S(1)} %get-tuple-element.1816, f32[32]{0:T(128)S(1)} %get-tuple-element.1817, f32[32]{0:T(128)S(1)} %get-tuple-element.1818), channel_id=1, replica_groups=mesh['gx_0'=4,'gx_1'=2,'gy'=8,'gz_0'=4,'gz_1'=2] {'gz_1'}, use_global_device_ids=true, to_apply=%region_24.25 | all-reduce | flops 96 | bytes 768 | tf_op jit(solution)/shard_map/psum | solution.py:36
  432.1 2.5 convolution_add_fusion
  (340 shorter events, 139.8 us)
Async XLA Ops:
  7.2 16.8 %copy-start = (bf16[256,128]{1,0:T(8,128)(2,1)S(1)}, bf16[256,128]{1,0:T(8,128)(2,1)}, u32[]{:S(2)}) copy-start(bf16[256,128]{1,0:T(8,128)(2,1)} %param.16) | copy-start | bytes 196612
  10.4 21.9 %all-to-all-start.1 = ((f32[1,32,8]{1,0,2:T(1,128)}), f32[1,32,8]{1,0,2:T(1,128)S(1)}, u32[]{:S(2)}, u32[]{:S(2)}) async-start(f32[1,32,8]{1,0,2:T(1,128)} %broadcast_in_dim.210), calls=%async_computation.1 | async-start | bytes 8192 | tf_op jit(solution)/shard_map/all_to_all | solution.py:124
  23.8 1.2 copy-start.1
  32.3 34.3 %all-to-all-start = ((f32[1,32,64,128]{3,1,0,2:T(8,128)}), f32[1,32,64,128]{3,1,0,2:T(8,128)S(1)}, u32[]{:S(2)}, u32[]{:S(2)}) async-start(f32[1,32,64,128]{3,1,0,2:T(8,128)} %copy.171), calls=%async_computation | async-start | bytes 2097152 | tf_op jit(solution)/shard_map/all_to_all | solution.py:125
  36.3 69.5 %all-gather.5.cloned.1.call-start = ((), (), s32[]{:S(2)}) async-start(), calls=%async_computation.4 | async-start | bytes 1179648 | tf_op jit(solution)/shard_map/all_gather | solution.py:24
  37.0 31.3 %copy-start.18 = (f32[32]{0:T(128)}, f32[32]{0:T(128)S(1)}, u32[]{:S(2)}) copy-start(f32[32]{0:T(128)S(1)} %get-tuple-element.1883) | copy-start | bytes 388
  37.4 30.9 %copy-start.20 = (f32[32]{0:T(128)}, f32[32]{0:T(128)S(1)}, u32[]{:S(2)}) copy-start(f32[32]{0:T(128)S(1)} %get-tuple-element.1874) | copy-start | bytes 388
  37.4 30.9 %copy-start.22 = (f32[32]{0:T(128)}, f32[32]{0:T(128)S(1)}, u32[]{:S(2)}) copy-start(f32[32]{0:T(128)S(1)} %get-tuple-element.1870) | copy-start | bytes 388
  37.4 30.9 %copy-start.24 = (f32[32]{0:T(128)}, f32[32]{0:T(128)S(1)}, u32[]{:S(2)}) copy-start(f32[32]{0:T(128)S(1)} %get-tuple-element.1872) | copy-start | bytes 388
  37.4 35.2 %copy-start.31 = (f32[32]{0:T(128)S(1)}, f32[32]{0:T(128)}, u32[]{:S(2)}) copy-start(f32[32]{0:T(128)} %param.18) | copy-start | bytes 388
  37.5 35.8 %copy-start.41 = (f32[32]{0:T(128)S(1)}, f32[32]{0:T(128)}, u32[]{:S(2)}) copy-start(f32[32]{0:T(128)} %param.17) | copy-start | bytes 388
  68.3 7.7 %copy-start.42 = (f32[32]{0:T(128)S(1)}, f32[32]{0:T(128)}, u32[]{:S(2)}) copy-start(f32[32]{0:T(128)} %param.19) | copy-start | bytes 388
  68.3 8.3 %copy-start.9 = (bf16[256,128]{1,0:T(8,128)(2,1)S(1)}, bf16[256,128]{1,0:T(8,128)(2,1)}, u32[]{:S(2)}) copy-start(bf16[256,128]{1,0:T(8,128)(2,1)} %param.15) | copy-start | bytes 196612
  68.3 65.7 %all-to-all-start.3 = ((bf16[8,32,8,128]{3,2,1,0:T(8,128)(2,1)}), bf16[8,32,8,128]{3,2,1,0:T(8,128)(2,1)}, u32[]{:S(2)}, u32[]{:S(2)}) async-start(bf16[8,32,8,128]{3,2,1,0:T(8,128)(2,1)} %param.20), calls=%async_computation.3 | async-start | bytes 1048576 | tf_op jit(solution)/shard_map/all_to_all | solution.py:106
  93.6 14.0 %copy-start.14 = (f32[32]{0:T(128)}, f32[32]{0:T(128)S(1)}, u32[]{:S(2)}) copy-start(f32[32]{0:T(128)S(1)} %get-tuple-element.1878) | copy-start | bytes 388
  93.6 14.0 %copy-start.15 = (f32[32]{0:T(128)}, f32[32]{0:T(128)S(1)}, u32[]{:S(2)}) copy-start(f32[32]{0:T(128)S(1)} %get-tuple-element.1879) | copy-start | bytes 388
  93.6 14.0 %copy-start.16 = (f32[32]{0:T(128)}, f32[32]{0:T(128)S(1)}, u32[]{:S(2)}) copy-start(f32[32]{0:T(128)S(1)} %get-tuple-element.1881) | copy-start | bytes 388
  93.6 14.0 %copy-start.17 = (f32[32]{0:T(128)}, f32[32]{0:T(128)S(1)}, u32[]{:S(2)}) copy-start(f32[32]{0:T(128)S(1)} %get-tuple-element.1882) | copy-start | bytes 388
  95.4 14.4 %copy-start.21 = (f32[32]{0:T(128)}, f32[32]{0:T(128)S(1)}, u32[]{:S(2)}) copy-start(f32[32]{0:T(128)S(1)} %get-tuple-element.1889) | copy-start | bytes 388
  103.6 4.0 copy-start.26
  103.6 6.2 %copy-start.27 = (f32[32]{0:T(128)}, f32[32]{0:T(128)S(1)}, u32[]{:S(2)}) copy-start(f32[32]{0:T(128)S(1)} %bitcast_multiply_fusion.17) | copy-start | bytes 388
  105.8 20.7 %copy-start.5 = (f32[8,32,8,128]{3,2,1,0:T(8,128)S(1)}, f32[8,32,8,128]{3,2,1,0:T(8,128)}, u32[]{:S(2)}) copy-start(f32[8,32,8,128]{3,2,1,0:T(8,128)} %all-gather.5.cloned.1.call-done) | copy-start | bytes 3145732
  105.8 20.7 %copy-start.33 = (f32[32]{0:T(128)S(1)}, f32[32]{0:T(128)}, u32[]{:S(2)}) copy-start(f32[32]{0:T(128)} %get-tuple-element.1844) | copy-start | bytes 388
  105.8 20.7 %copy-start.34 = (f32[32]{0:T(128)S(1)}, f32[32]{0:T(128)}, u32[]{:S(2)}) copy-start(f32[32]{0:T(128)} %get-tuple-element.1845) | copy-start | bytes 388
  105.8 20.7 %copy-start.35 = (f32[32]{0:T(128)S(1)}, f32[32]{0:T(128)}, u32[]{:S(2)}) copy-start(f32[32]{0:T(128)} %get-tuple-element.1884) | copy-start | bytes 388
  105.8 20.7 %copy-start.36 = (f32[32]{0:T(128)S(1)}, f32[32]{0:T(128)}, u32[]{:S(2)}) copy-start(f32[32]{0:T(128)} %get-tuple-element.1885) | copy-start | bytes 388
  105.8 20.7 %copy-start.37 = (f32[32]{0:T(128)S(1)}, f32[32]{0:T(128)}, u32[]{:S(2)}) copy-start(f32[32]{0:T(128)} %get-tuple-element.1886) | copy-start | bytes 388
  105.9 20.7 %copy-start.38 = (f32[32]{0:T(128)S(1)}, f32[32]{0:T(128)}, u32[]{:S(2)}) copy-start(f32[32]{0:T(128)} %get-tuple-element.1887) | copy-start | bytes 388
  107.6 21.2 %copy-start.30 = (f32[32]{0:T(128)S(1)}, f32[32]{0:T(128)}, u32[]{:S(2)}) copy-start(f32[32]{0:T(128)} %get-tuple-element.1839) | copy-start | bytes 388
  107.6 21.9 %copy-start.7 = (f32[1,32,8,128]{3,2,1,0:T(8,128)S(1)}, f32[1,32,8,128]{3,2,1,0:T(8,128)}, u32[]{:S(2)}) copy-start(f32[1,32,8,128]{3,2,1,0:T(8,128)} %get-tuple-element.1850) | copy-start | bytes 393220
  107.6 21.9 %copy-start.25 = (f32[32]{0:T(128)S(1)}, f32[32]{0:T(128)}, u32[]{:S(2)}) copy-start(f32[32]{0:T(128)} %copy-done.24) | copy-start | bytes 388
  107.7 21.9 %copy-start.40 = (f32[32]{0:T(128)S(1)}, f32[32]{0:T(128)}, u32[]{:S(2)}) copy-start(f32[32]{0:T(128)} %get-tuple-element.1840) | copy-start | bytes 388
  109.8 20.5 %copy-start.29 = (f32[32]{0:T(128)S(1)}, f32[32]{0:T(128)}, u32[]{:S(2)}) copy-start(f32[32]{0:T(128)} %get-tuple-element.1841) | copy-start | bytes 388
  109.9 21.2 %copy-start.6 = (f32[1,32,8,128]{3,2,1,0:T(8,128)S(1)}, f32[1,32,8,128]{3,2,1,0:T(8,128)}, u32[]{:S(2)}) copy-start(f32[1,32,8,128]{3,2,1,0:T(8,128)} %get-tuple-element.1851) | copy-start | bytes 393220
  109.9 21.1 %copy-start.23 = (f32[32]{0:T(128)S(1)}, f32[32]{0:T(128)}, u32[]{:S(2)}) copy-start(f32[32]{0:T(128)} %copy-done.22) | copy-start | bytes 388
  110.0 21.1 %copy-start.39 = (f32[32]{0:T(128)S(1)}, f32[32]{0:T(128)}, u32[]{:S(2)}) copy-start(f32[32]{0:T(128)} %get-tuple-element.1842) | copy-start | bytes 388
  126.5 5.3 %copy-start.28 = (f32[32]{0:T(128)S(1)}, f32[32]{0:T(128)}, u32[]{:S(2)}) copy-start(f32[32]{0:T(128)} %get-tuple-element.1843) | copy-start | bytes 388
  126.5 6.1 %copy-start.19 = (f32[32]{0:T(128)S(1)}, f32[32]{0:T(128)}, u32[]{:S(2)}) copy-start(f32[32]{0:T(128)} %copy-done.18) | copy-start | bytes 388
  126.6 6.1 %copy-start.32 = (f32[32]{0:T(128)S(1)}, f32[32]{0:T(128)}, u32[]{:S(2)}) copy-start(f32[32]{0:T(128)} %get-tuple-element.1866) | copy-start | bytes 388
  134.0 11.7 %copy-start.8 = (f32[256,32]{0,1:T(8,128)S(1)}, f32[256,32]{0,1:T(8,128)}, u32[]{:S(2)}) copy-start(f32[256,32]{0,1:T(8,128)} %param.14) | copy-start | bytes 98308
  134.1 76.5 %all-to-all-start.2 = ((f32[8,32,8,128]{3,2,1,0:T(8,128)}), f32[8,32,8,128]{3,2,1,0:T(8,128)}, u32[]{:S(2)}, u32[]{:S(2)}) async-start(f32[8,32,8,128]{3,2,1,0:T(8,128)} %constant_dynamic-update-slice_fusion.3), calls=%async_computation.2 | async-start | bytes 2097152 | tf_op jit(solution)/shard_map/all_to_all | solution.py:147
  203.1 1.4 copy-start.10
  207.6 3.0 copy-start.3
  216.8 0.6 copy-start.11
  246.7 3.8 copy-start.13
  250.4 5.6 %copy-start.12 = (f32[4,8]{0,1:T(8,128)S(1)}, f32[4,8]{0,1:T(8,128)}, u32[]{:S(2)}) copy-start(f32[4,8]{0,1:T(8,128)} %copy-done.11) | copy-start | bytes 388 | tf_op jit(solution)/shard_map/transpose(jvp())/while
  256.1 0.6 copy-start.11
  286.0 3.8 copy-start.13
  289.7 5.7 %copy-start.12 = (f32[4,8]{0,1:T(8,128)S(1)}, f32[4,8]{0,1:T(8,128)}, u32[]{:S(2)}) copy-start(f32[4,8]{0,1:T(8,128)} %copy-done.11) | copy-start | bytes 388 | tf_op jit(solution)/shard_map/transpose(jvp())/while
  295.3 0.6 copy-start.11
  325.3 3.8 copy-start.13
  329.0 5.7 %copy-start.12 = (f32[4,8]{0,1:T(8,128)S(1)}, f32[4,8]{0,1:T(8,128)}, u32[]{:S(2)}) copy-start(f32[4,8]{0,1:T(8,128)} %copy-done.11) | copy-start | bytes 388 | tf_op jit(solution)/shard_map/transpose(jvp())/while
  334.7 0.6 copy-start.11
  364.6 3.8 copy-start.13
  368.3 5.7 %copy-start.12 = (f32[4,8]{0,1:T(8,128)S(1)}, f32[4,8]{0,1:T(8,128)}, u32[]{:S(2)}) copy-start(f32[4,8]{0,1:T(8,128)} %copy-done.11) | copy-start | bytes 388 | tf_op jit(solution)/shard_map/transpose(jvp())/while
  374.0 58.1 %copy-start.2 = (f32[4,256,8,64]{1,3,2,0:T(8,128)S(1)}, f32[4,256,8,64]{1,3,2,0:T(8,128)}, u32[]{:S(2)}) copy-start(f32[4,256,8,64]{1,3,2,0:T(8,128)} %get-tuple-element.1033) | copy-start | bytes 6291460
  374.0 58.1 %copy-start.4 = (bf16[8,32,8,128]{3,2,0,1:T(8,128)(2,1)S(1)}, bf16[8,32,8,128]{3,2,0,1:T(8,128)(2,1)}, u32[]{:S(2)}) copy-start(bf16[8,32,8,128]{3,2,0,1:T(8,128)(2,1)} %copy-done.3) | copy-start | bytes 1572868
Sparse Core Ops, SparseCore 0:
  68.4 37.3 all-gather.4
where the time goes:
time: 445 us; the launch traced here: 441 us
  local copies, waits for them, and re-layouts  99.1 us (22%)
  other arithmetic  98.9 us (22%)
  blocking collectives  95.8 us (22%)
  matrix products  70.4 us (16%)
  waiting for transfers between devices  35.7 us (8%)
  starting transfers between devices  26.6 us (6%)
  between operations  14.6 us (3%)
    psum x5, blocking collectives, by_axis(): array = lax.psum(array, axis)  50.4 us
    all_gather x5, blocking collectives, carried_in(): pieces = jax.tree.map(lambda part: lax.all_gather(part, axis), so_far)  45.4 us
    dot_general x8, matrix products, block_forward(): inner = jnp.einsum('hts,shp->thp', mix, inputs, precision=highest)  40.7 us
    dynamic_update_slice x36, local copies, waits for them, and re-layouts, span_forward(): lax.map(one_block, (grouped, raw_g, read_g, decay_log.reshape(blocks, blo...  32.7 us
    dynamic_update_slice x24, other arithmetic, span_forward(): lax.map(one_block, (grouped, raw_g, read_g, decay_log.reshape(blocks, blo...  30.3 us
    all_to_all x1, waiting for transfers between devices, local(): lax.all_to_all(local_term[None], GZ, split_axis=2, concat_axis=0, tiled=T...  29.1 us
    another operation x33, other arithmetic  27.8 us
    dot_general x8, matrix products, block_forward(): jnp.einsum('sh,shp,sn->hpn', tail, inputs, b_mat, precision=highest)  21.1 us
  transfers between devices with their start and end apart: 5, of which 3 were waited for; matrix products, arithmetic and copies ran while one was open for 20% of the time, Pallas kernels for 0%

commit v1 on v0

--- a/solution.py
+++ b/solution.py
@@ -122,7 +122,12 @@
     spread = jnp.broadcast_to(decays[None, :, None], (1, heads, group))
     got_decay, got_term = (
         lax.all_to_all(spread, GZ, split_axis=2, concat_axis=0, tiled=True),
-        lax.all_to_all(local_term[None], GZ, split_axis=2, concat_axis=0, tiled=True),
+        jnp.concatenate(
+            lax.all_to_all(
+                jnp.stack(jnp.split(local_term[None], lax.axis_size(GZ), axis=2)), GZ, 0, 0
+            ),
+            axis=0,
+        ),
     )
     got_decay = got_decay[:, :, 0]
     slice_width = got_term.shape[2]

time: 445 us -> 449 us (level)
    unnamed x82 -> x93, local copies, waits for them, and re-layouts: 3.92 us -> 8.61 us
    another operation x30 -> x31, local copies, waits for them, and re-layouts: 15.2 us -> 15.9 us
  transfers between devices with their start and end apart: 5 -> 5, of which waited for: 3 -> 3; matrix products, arithmetic and copies ran while one was open for 20% -> 21% of each run, Pallas kernels for 0% -> 0%
where the time goes in v1:
time: 449 us; the launch traced here: 445 us
  local copies, waits for them, and re-layouts  101 us (22%)
  other arithmetic  99 us (22%)
  blocking collectives  96.2 us (21%)
  matrix products  70.4 us (16%)
  waiting for transfers between devices  32.7 us (7%)
  starting transfers between devices  30.4 us (7%)
  between operations  14.6 us (3%)
    psum x5, blocking collectives, by_axis(): array = lax.psum(array, axis)  50.6 us
    all_gather x5, blocking collectives, carried_in(): pieces = jax.tree.map(lambda part: lax.all_gather(part, axis), so_far)  45.6 us
    dot_general x8, matrix products, block_forward(): inner = jnp.einsum('hts,shp->thp', mix, inputs, precision=highest)  40.7 us
    dynamic_update_slice x36, local copies, waits for them, and re-layouts, span_forward(): lax.map(one_block, (grouped, raw_g, read_g, decay_log.reshape(blocks, blo...  32.8 us
    dynamic_update_slice x24, other arithmetic, span_forward(): lax.map(one_block, (grouped, raw_g, read_g, decay_log.reshape(blocks, blo...  30.4 us
    all_to_all x1, waiting for transfers between devices, local(): lax.all_to_all(jnp.stack(jnp.split(local_term[None], lax.axis_size(GZ), a...  29 us
    another operation x33, other arithmetic  27.7 us
    dot_general x8, matrix products, block_forward(): jnp.einsum('sh,shp,sn->hpn', tail, inputs, b_mat, precision=highest)  21.1 us
  transfers between devices with their start and end apart: 5, of which 3 were waited for; matrix products, arithmetic and copies ran while one was open for 21% of the time, Pallas kernels for 0%

profile of v1, /device:TPU:64, one launch (start us, length us, event | category | flops | bytes accessed | tf_op | source)
XLA Modules:
  0.0 445.0 jit_solution(16766089574438664800)
XLA Ops:
  10.4 11.8 %all-to-all-start.1 = ((f32[1,32,8]{1,0,2:T(1,128)}), f32[1,32,8]{1,0,2:T(1,128)S(1)}, u32[]{:S(2)}, u32[]{:S(2)}) async-start(f32[1,32,8]{1,0,2:T(1,128)} %broadcast_in_dim.210), calls=%async_computation.1 | async-start | bytes 8192 | tf_op jit(solution)/shard_map/all_to_all | solution.py:124
  22.4 1.5 copy.91
  30.5 1.8 all-to-all-done.1
  32.3 7.9 %all-to-all-start = ((f32[8,1,32,8,128]{4,3,2,1,0:T(8,128)}), f32[8,1,32,8,128]{4,3,2,1,0:T(8,128)S(1)}, u32[]{:S(2)}, u32[]{:S(2)}) async-start(f32[8,1,32,8,128]{4,3,2,1,0:T(8,128)} %fusion.85), calls=%async_computation | async-start | bytes 2097152 | tf_op jit(solution)/shard_map/all_to_all | solution.py:126
  41.5 29.0 %all-to-all-done = f32[8,1,32,8,128]{4,3,2,1,0:T(8,128)S(1)} async-done(((f32[8,1,32,8,128]{4,3,2,1,0:T(8,128)}), f32[8,1,32,8,128]{4,3,2,1,0:T(8,128)S(1)}, u32[]{:S(2)}, u32[]{:S(2)}) %all-to-all-start) | async-done | bytes 1048608 | tf_op jit(solution)/shard_map/all_to_all | solution.py:126
  71.6 4.3 all-to-all-start.3
  76.8 1.6 copy.87
  79.3 16.8 %all-gather = f32[8,1,32,1]{2,3,1,0:T(1,128)S(1)} all-gather(f32[1,1,32,1]{2,3,1,0:T(1,128)S(1)} %get-tuple-element.1740), channel_id=2, replica_groups=mesh['gx_0'=4,'gx_1'=2,'gy'=8,'gz_0'=4,'gz_1'=2] {'gy'}, dimensions={0}, use_global_device_ids=true | all-gather | bytes 1152 | tf_op jit(solution)/shard_map/all_gather | solution.py:24
  96.1 1.8 all-gather.1
  97.9 8.2 %all-gather.2 = f32[4,1,32]{2,1,0:T(1,128)S(1)} all-gather(f32[1,1,32]{2,1,0:T(1,128)S(1)} %get-tuple-element.1760), channel_id=1, replica_groups=mesh['gx_0'=4,'gx_1'=2,'gy'=8,'gz_0'=4,'gz_1'=2] {'gx_0'}, dimensions={0}, use_global_device_ids=true | all-gather | bytes 640 | tf_op jit(solution)/shard_map/all_gather | solution.py:24
  107.3 1.9 all-gather.5.cloned.1.call-done
  109.2 1.7 slice_add_fusion.6
  111.0 2.1 all_gather.28
  113.3 16.7 %all_gather.29 = f32[4,32,8,128]{3,2,1,0:T(8,128)S(1)} all-gather(f32[1,32,8,128]{3,2,1,0:T(8,128)S(1)} %slice_add_fusion.4), channel_id=1, replica_groups=mesh['gx_0'=4,'gx_1'=2,'gy'=8,'gz_0'=4,'gz_1'=2] {'gx_0'}, dimensions={0}, use_global_device_ids=true | all-gather | bytes 655360 | tf_op jit(solution)/shard_map/all_gather | solution.py:24
  130.1 2.2 add_dynamic-update-slice_fusion.6
  137.6 6.2 %all-to-all-start.2 = ((f32[8,32,8,128]{3,2,1,0:T(8,128)}), f32[8,32,8,128]{3,2,1,0:T(8,128)}, u32[]{:S(2)}, u32[]{:S(2)}) async-start(f32[8,32,8,128]{3,2,1,0:T(8,128)} %constant_dynamic-update-slice_fusion.3), calls=%async_computation.2 | async-start | bytes 2097152 | tf_op jit(solution)/shard_map/all_to_all | solution.py:152
  143.9 1.5 broadcast.740.clone.1
  149.1 57.5 %while.75 = (s32[]{:T(128)}, f32[4,256,8]{1,2,0:T(8,128)}, f32[4,8]{1,0:T(4,128)}, f32[4,1,8]{2,1,0:T(1,128)}, f32[4,256,8]{1,2,0:T(8,128)}, /*index=5*/f32[4,8,...) while((s32[]{:T(128)}, f32[4,256,8]{1,2,0:T(8,128)}, ...), condition=%wide.region_5.6_spmd.clone.clone, body=%wide.region_2.5_spmd.clone.clone.sunk | while | flops 3090474 | bytes 14180141 | solution.py:75
  150.7 4.2 multiply_dynamic-update-slice_fusion.4
  165.1 4.0 multiply_dynamic-update-slice_fusion.4
  179.5 4.1 multiply_dynamic-update-slice_fusion.4
  193.9 4.0 multiply_dynamic-update-slice_fusion.4
  212.1 1.8 convolution_bitcast_fusion.2
  213.9 2.3 copy.95
  216.3 1.5 broadcast.740
  220.1 157.2 %while.76 = (s32[]{:T(128)}, f32[256,256]{1,0:T(8,128)S(1)}, f32[256,128]{1,0:T(8,128)}, bf16[4,256,8,64]{1,3,2,0:T(8,128)(2,1)}, f32[4,256,8]{1,2,0:T(8,128)}, ...) while((s32[]{:T(128)}, f32[256,256]{1,0:T(8,128)S(1)}, ...), condition=%wide.region_19.20_spmd.clone.clone, body=%wide.region_6.19_spmd.clone.clone.sunk | while | flops 1215725568 | bytes 18326480 | solution.py:75
  220.7 2.5 fusion.160
  225.4 6.5 %fusion.158 = (f32[8,256]{1,0:T(8,128)}, f32[8,256]{1,0:T(8,128)}, f32[256,256]{1,0:T(8,128)S(1)}, f32[8,256]{1,0:T(8,128)}) fusion(f32[4,8,256,256]{3,2,1,0:T(8,128)} %get-tuple-element.2346, s32[]{:T(128)S(6)} %sub.146, f32[256,256]{1,0:T(8,128)S(1)} %bitcast.592, f32[8,256]{1,0:T(8,128)S(1)} %dynamic-slice_bitcast_fusion.6, ...), kind=kOutput, calls=%fused_computation.87.clone.1 | convolution fusion | flops 408348672 | bytes 7964160 | tf_op jit(solution)/shard_map/transpose(jvp())/while/body/eval_jaxpr/hts,shp->thp/dot_general | solution.py:50
  231.9 1.7 fusion.165
  235.6 1.4 fusion.167
  237.1 3.1 reduce-window.62
  243.4 1.4 fusion.168
  250.0 3.7 fusion.162
  256.6 2.8 fusion.159
  260.0 2.5 fusion.160
  264.7 6.5 %fusion.158 = (f32[8,256]{1,0:T(8,128)}, f32[8,256]{1,0:T(8,128)}, f32[256,256]{1,0:T(8,128)S(1)}, f32[8,256]{1,0:T(8,128)}) fusion(f32[4,8,256,256]{3,2,1,0:T(8,128)} %get-tuple-element.2346, s32[]{:T(128)S(6)} %sub.146, f32[256,256]{1,0:T(8,128)S(1)} %bitcast.592, f32[8,256]{1,0:T(8,128)S(1)} %dynamic-slice_bitcast_fusion.6, ...), kind=kOutput, calls=%fused_computation.87.clone.1 | convolution fusion | flops 408348672 | bytes 7964160 | tf_op jit(solution)/shard_map/transpose(jvp())/while/body/eval_jaxpr/hts,shp->thp/dot_general | solution.py:50
  271.1 1.7 fusion.165
  276.3 3.1 reduce-window.62
  282.7 1.4 fusion.168
  289.3 3.7 fusion.162
  295.9 2.8 fusion.159
  299.3 2.5 fusion.160
  304.0 6.5 %fusion.158 = (f32[8,256]{1,0:T(8,128)}, f32[8,256]{1,0:T(8,128)}, f32[256,256]{1,0:T(8,128)S(1)}, f32[8,256]{1,0:T(8,128)}) fusion(f32[4,8,256,256]{3,2,1,0:T(8,128)} %get-tuple-element.2346, s32[]{:T(128)S(6)} %sub.146, f32[256,256]{1,0:T(8,128)S(1)} %bitcast.592, f32[8,256]{1,0:T(8,128)S(1)} %dynamic-slice_bitcast_fusion.6, ...), kind=kOutput, calls=%fused_computation.87.clone.1 | convolution fusion | flops 408348672 | bytes 7964160 | tf_op jit(solution)/shard_map/transpose(jvp())/while/body/eval_jaxpr/hts,shp->thp/dot_general | solution.py:50
  310.5 1.7 fusion.165
  314.2 1.4 fusion.167
  315.7 3.1 reduce-window.62
  322.1 1.4 fusion.168
  328.6 3.7 fusion.162
  335.3 2.8 fusion.159
  338.7 2.5 fusion.160
  343.4 6.5 %fusion.158 = (f32[8,256]{1,0:T(8,128)}, f32[8,256]{1,0:T(8,128)}, f32[256,256]{1,0:T(8,128)S(1)}, f32[8,256]{1,0:T(8,128)}) fusion(f32[4,8,256,256]{3,2,1,0:T(8,128)} %get-tuple-element.2346, s32[]{:T(128)S(6)} %sub.146, f32[256,256]{1,0:T(8,128)S(1)} %bitcast.592, f32[8,256]{1,0:T(8,128)S(1)} %dynamic-slice_bitcast_fusion.6, ...), kind=kOutput, calls=%fused_computation.87.clone.1 | convolution fusion | flops 408348672 | bytes 7964160 | tf_op jit(solution)/shard_map/transpose(jvp())/while/body/eval_jaxpr/hts,shp->thp/dot_general | solution.py:50
  349.8 1.7 fusion.165
  355.0 3.1 reduce-window.62
  361.4 1.4 fusion.168
  367.9 3.7 fusion.162
  374.6 2.8 fusion.159
  380.9 1.9 convolution_add_fusion.1
  382.9 2.3 copy.98
  385.1 11.9 %all-reduce.4 = (f32[32]{0:T(128)S(1)}, f32[32]{0:T(128)S(1)}, f32[32]{0:T(128)S(1)}) all-reduce(f32[32]{0:T(128)S(1)} %reshape.896, f32[32]{0:T(128)S(1)} %reshape.897, f32[32]{0:T(128)S(1)} %reshape.898), channel_id=1, replica_groups=mesh['gx_0'=4,'gx_1'=2,'gy'=8,'gz_0'=4,'gz_1'=2] {'gx_0'}, use_global_device_ids=true, to_apply=%region_20.21 | all-reduce | flops 96 | bytes 768 | tf_op jit(solution)/shard_map/psum | solution.py:36
  397.0 2.5 all-reduce.6
  399.5 15.9 %all-reduce.2 = (f32[32]{0:T(128)S(1)}, f32[32]{0:T(128)S(1)}, f32[32]{0:T(128)S(1)}) all-reduce(f32[32]{0:T(128)S(1)} %get-tuple-element.1697, f32[32]{0:T(128)S(1)} %get-tuple-element.1698, f32[32]{0:T(128)S(1)} %get-tuple-element.1699), channel_id=1, replica_groups=mesh['gx_0'=4,'gx_1'=2,'gy'=8,'gz_0'=4,'gz_1'=2] {'gy'}, use_global_device_ids=true, to_apply=%region_22.23 | all-reduce | flops 96 | bytes 768 | tf_op jit(solution)/shard_map/psum | solution.py:36
  415.4 10.9 %all-reduce.3 = (f32[32]{0:T(128)S(1)}, f32[32]{0:T(128)S(1)}, f32[32]{0:T(128)S(1)}) all-reduce(f32[32]{0:T(128)S(1)} %get-tuple-element.1685, f32[32]{0:T(128)S(1)} %get-tuple-element.1686, f32[32]{0:T(128)S(1)} %get-tuple-element.1687), channel_id=1, replica_groups=mesh['gx_0'=4,'gx_1'=2,'gy'=8,'gz_0'=4,'gz_1'=2] {'gz_0'}, use_global_device_ids=true, to_apply=%region_23.24 | all-reduce | flops 96 | bytes 768 | tf_op jit(solution)/shard_map/psum | solution.py:36
  426.3 9.3 %all-reduce.5 = (f32[32]{0:T(128)}, f32[32]{0:T(128)}, f32[32]{0:T(128)}) all-reduce(f32[32]{0:T(128)S(1)} %get-tuple-element.1688, f32[32]{0:T(128)S(1)} %get-tuple-element.1689, f32[32]{0:T(128)S(1)} %get-tuple-element.1690), channel_id=1, replica_groups=mesh['gx_0'=4,'gx_1'=2,'gy'=8,'gz_0'=4,'gz_1'=2] {'gz_1'}, use_global_device_ids=true, to_apply=%region_24.25 | all-reduce | flops 96 | bytes 768 | tf_op jit(solution)/shard_map/psum | solution.py:36
  435.7 2.5 convolution_add_fusion
  (350 shorter events, 143.8 us)
Async XLA Ops:
  7.2 16.8 %copy-start = (bf16[256,128]{1,0:T(8,128)(2,1)S(1)}, bf16[256,128]{1,0:T(8,128)(2,1)}, u32[]{:S(2)}) copy-start(bf16[256,128]{1,0:T(8,128)(2,1)} %param.16) | copy-start | bytes 196612
  10.4 21.9 %all-to-all-start.1 = ((f32[1,32,8]{1,0,2:T(1,128)}), f32[1,32,8]{1,0,2:T(1,128)S(1)}, u32[]{:S(2)}, u32[]{:S(2)}) async-start(f32[1,32,8]{1,0,2:T(1,128)} %broadcast_in_dim.210), calls=%async_computation.1 | async-start | bytes 8192 | tf_op jit(solution)/shard_map/all_to_all | solution.py:124
  23.8 1.2 copy-start.1
  30.5 45.6 %copy-start.33 = (f32[32]{0:T(128)S(1)}, f32[32]{0:T(128)}, u32[]{:S(2)}) copy-start(f32[32]{0:T(128)} %param.18) | copy-start | bytes 388
  30.5 46.2 %copy-start.43 = (f32[32]{0:T(128)S(1)}, f32[32]{0:T(128)}, u32[]{:S(2)}) copy-start(f32[32]{0:T(128)} %param.17) | copy-start | bytes 388
  30.5 46.3 %copy-start.8 = (bf16[256,2048]{1,0:T(8,128)(2,1)S(1)}, bf16[256,2048]{1,0:T(8,128)(2,1)}, u32[]{:S(2)}) copy-start(bf16[256,2048]{1,0:T(8,128)(2,1)} %param.13) | copy-start | bytes 3145732
  32.3 38.2 %all-to-all-start = ((f32[8,1,32,8,128]{4,3,2,1,0:T(8,128)}), f32[8,1,32,8,128]{4,3,2,1,0:T(8,128)S(1)}, u32[]{:S(2)}, u32[]{:S(2)}) async-start(f32[8,1,32,8,128]{4,3,2,1,0:T(8,128)} %fusion.85), calls=%async_computation | async-start | bytes 2097152 | tf_op jit(solution)/shard_map/all_to_all | solution.py:126
  40.2 68.9 %all-gather.5.cloned.1.call-start = ((), (), s32[]{:S(2)}) async-start(), calls=%async_computation.4 | async-start | bytes 1179648 | tf_op jit(solution)/shard_map/all_gather | solution.py:24
  40.9 37.5 %copy-start.19 = (f32[32]{0:T(128)}, f32[32]{0:T(128)S(1)}, u32[]{:S(2)}) copy-start(f32[32]{0:T(128)S(1)} %get-tuple-element.1755) | copy-start | bytes 388
  41.5 36.9 %copy-start.21 = (f32[32]{0:T(128)}, f32[32]{0:T(128)S(1)}, u32[]{:S(2)}) copy-start(f32[32]{0:T(128)S(1)} %get-tuple-element.1746) | copy-start | bytes 388
  41.5 36.9 %copy-start.24 = (f32[32]{0:T(128)}, f32[32]{0:T(128)S(1)}, u32[]{:S(2)}) copy-start(f32[32]{0:T(128)S(1)} %get-tuple-element.1742) | copy-start | bytes 388
  41.5 36.9 %copy-start.26 = (f32[32]{0:T(128)}, f32[32]{0:T(128)S(1)}, u32[]{:S(2)}) copy-start(f32[32]{0:T(128)S(1)} %get-tuple-element.1744) | copy-start | bytes 388
  71.6 6.8 %copy-start.44 = (f32[32]{0:T(128)S(1)}, f32[32]{0:T(128)}, u32[]{:S(2)}) copy-start(f32[32]{0:T(128)} %param.19) | copy-start | bytes 388
  71.6 7.5 %copy-start.10 = (bf16[256,128]{1,0:T(8,128)(2,1)S(1)}, bf16[256,128]{1,0:T(8,128)(2,1)}, u32[]{:S(2)}) copy-start(bf16[256,128]{1,0:T(8,128)(2,1)} %param.15) | copy-start | bytes 196612
  71.6 66.0 %all-to-all-start.3 = ((bf16[8,32,8,128]{3,2,1,0:T(8,128)(2,1)}), bf16[8,32,8,128]{3,2,1,0:T(8,128)(2,1)}, u32[]{:S(2)}, u32[]{:S(2)}) async-start(bf16[8,32,8,128]{3,2,1,0:T(8,128)(2,1)} %param.20), calls=%async_computation.3 | async-start | bytes 1048576 | tf_op jit(solution)/shard_map/all_to_all | solution.py:106
  96.1 14.8 %copy-start.15 = (f32[32]{0:T(128)}, f32[32]{0:T(128)S(1)}, u32[]{:S(2)}) copy-start(f32[32]{0:T(128)S(1)} %get-tuple-element.1750) | copy-start | bytes 388
  96.1 14.8 %copy-start.16 = (f32[32]{0:T(128)}, f32[32]{0:T(128)S(1)}, u32[]{:S(2)}) copy-start(f32[32]{0:T(128)S(1)} %get-tuple-element.1751) | copy-start | bytes 388
  96.1 14.8 %copy-start.17 = (f32[32]{0:T(128)}, f32[32]{0:T(128)S(1)}, u32[]{:S(2)}) copy-start(f32[32]{0:T(128)S(1)} %get-tuple-element.1753) | copy-start | bytes 388
  96.1 14.8 %copy-start.18 = (f32[32]{0:T(128)}, f32[32]{0:T(128)S(1)}, u32[]{:S(2)}) copy-start(f32[32]{0:T(128)S(1)} %get-tuple-element.1754) | copy-start | bytes 388
  97.9 15.2 %copy-start.23 = (f32[32]{0:T(128)}, f32[32]{0:T(128)S(1)}, u32[]{:S(2)}) copy-start(f32[32]{0:T(128)S(1)} %get-tuple-element.1761) | copy-start | bytes 388
  106.1 4.8 %copy-start.28 = (f32[32]{0:T(128)}, f32[32]{0:T(128)S(1)}, u32[]{:S(2)}) copy-start(f32[32]{0:T(128)S(1)} %bitcast_multiply_fusion.15) | copy-start | bytes 388
  106.1 7.0 %copy-start.29 = (f32[32]{0:T(128)}, f32[32]{0:T(128)S(1)}, u32[]{:S(2)}) copy-start(f32[32]{0:T(128)S(1)} %bitcast_multiply_fusion.17) | copy-start | bytes 388
  109.1 20.9 %copy-start.5 = (f32[8,32,8,128]{3,2,1,0:T(8,128)S(1)}, f32[8,32,8,128]{3,2,1,0:T(8,128)}, u32[]{:S(2)}) copy-start(f32[8,32,8,128]{3,2,1,0:T(8,128)} %all-gather.5.cloned.1.call-done) | copy-start | bytes 3145732
  109.1 20.9 %copy-start.22 = (f32[32]{0:T(128)S(1)}, f32[32]{0:T(128)}, u32[]{:S(2)}) copy-start(f32[32]{0:T(128)} %copy-done.21) | copy-start | bytes 388
  109.1 20.9 %copy-start.35 = (f32[32]{0:T(128)S(1)}, f32[32]{0:T(128)}, u32[]{:S(2)}) copy-start(f32[32]{0:T(128)} %get-tuple-element.1716) | copy-start | bytes 388
  109.1 20.9 %copy-start.36 = (f32[32]{0:T(128)S(1)}, f32[32]{0:T(128)}, u32[]{:S(2)}) copy-start(f32[32]{0:T(128)} %get-tuple-element.1717) | copy-start | bytes 388
  109.1 20.9 %copy-start.37 = (f32[32]{0:T(128)S(1)}, f32[32]{0:T(128)}, u32[]{:S(2)}) copy-start(f32[32]{0:T(128)} %get-tuple-element.1756) | copy-start | bytes 388
  109.2 20.9 %copy-start.38 = (f32[32]{0:T(128)S(1)}, f32[32]{0:T(128)}, u32[]{:S(2)}) copy-start(f32[32]{0:T(128)} %get-tuple-element.1757) | copy-start | bytes 388
  109.2 20.9 %copy-start.39 = (f32[32]{0:T(128)S(1)}, f32[32]{0:T(128)}, u32[]{:S(2)}) copy-start(f32[32]{0:T(128)} %get-tuple-element.1758) | copy-start | bytes 388
  109.2 20.9 %copy-start.40 = (f32[32]{0:T(128)S(1)}, f32[32]{0:T(128)}, u32[]{:S(2)}) copy-start(f32[32]{0:T(128)} %get-tuple-element.1759) | copy-start | bytes 388
  110.9 21.4 %copy-start.32 = (f32[32]{0:T(128)S(1)}, f32[32]{0:T(128)}, u32[]{:S(2)}) copy-start(f32[32]{0:T(128)} %get-tuple-element.1711) | copy-start | bytes 388
  110.9 22.1 %copy-start.7 = (f32[1,32,8,128]{3,2,1,0:T(8,128)S(1)}, f32[1,32,8,128]{3,2,1,0:T(8,128)}, u32[]{:S(2)}) copy-start(f32[1,32,8,128]{3,2,1,0:T(8,128)} %get-tuple-element.1722) | copy-start | bytes 393220
  111.0 22.1 %copy-start.27 = (f32[32]{0:T(128)S(1)}, f32[32]{0:T(128)}, u32[]{:S(2)}) copy-start(f32[32]{0:T(128)} %copy-done.26) | copy-start | bytes 388
  111.0 22.1 %copy-start.42 = (f32[32]{0:T(128)S(1)}, f32[32]{0:T(128)}, u32[]{:S(2)}) copy-start(f32[32]{0:T(128)} %get-tuple-element.1712) | copy-start | bytes 388
  113.1 20.8 %copy-start.31 = (f32[32]{0:T(128)S(1)}, f32[32]{0:T(128)}, u32[]{:S(2)}) copy-start(f32[32]{0:T(128)} %get-tuple-element.1713) | copy-start | bytes 388
  113.3 21.4 %copy-start.6 = (f32[1,32,8,128]{3,2,1,0:T(8,128)S(1)}, f32[1,32,8,128]{3,2,1,0:T(8,128)}, u32[]{:S(2)}) copy-start(f32[1,32,8,128]{3,2,1,0:T(8,128)} %get-tuple-element.1723) | copy-start | bytes 393220
  113.3 21.4 %copy-start.25 = (f32[32]{0:T(128)S(1)}, f32[32]{0:T(128)}, u32[]{:S(2)}) copy-start(f32[32]{0:T(128)} %copy-done.24) | copy-start | bytes 388
  113.3 21.4 %copy-start.41 = (f32[32]{0:T(128)S(1)}, f32[32]{0:T(128)}, u32[]{:S(2)}) copy-start(f32[32]{0:T(128)} %get-tuple-element.1714) | copy-start | bytes 388
  130.1 5.4 %copy-start.30 = (f32[32]{0:T(128)S(1)}, f32[32]{0:T(128)}, u32[]{:S(2)}) copy-start(f32[32]{0:T(128)} %get-tuple-element.1715) | copy-start | bytes 388
  130.1 6.1 %copy-start.20 = (f32[32]{0:T(128)S(1)}, f32[32]{0:T(128)}, u32[]{:S(2)}) copy-start(f32[32]{0:T(128)} %copy-done.19) | copy-start | bytes 388
  130.1 6.1 %copy-start.34 = (f32[32]{0:T(128)S(1)}, f32[32]{0:T(128)}, u32[]{:S(2)}) copy-start(f32[32]{0:T(128)} %get-tuple-element.1738) | copy-start | bytes 388
  137.6 11.4 %copy-start.9 = (f32[256,32]{0,1:T(8,128)S(1)}, f32[256,32]{0,1:T(8,128)}, u32[]{:S(2)}) copy-start(f32[256,32]{0,1:T(8,128)} %param.14) | copy-start | bytes 98308
  137.6 76.3 %all-to-all-start.2 = ((f32[8,32,8,128]{3,2,1,0:T(8,128)}), f32[8,32,8,128]{3,2,1,0:T(8,128)}, u32[]{:S(2)}, u32[]{:S(2)}) async-start(f32[8,32,8,128]{3,2,1,0:T(8,128)} %constant_dynamic-update-slice_fusion.3), calls=%async_computation.2 | async-start | bytes 2097152 | tf_op jit(solution)/shard_map/all_to_all | solution.py:152
  206.5 1.4 copy-start.11
  211.0 3.0 copy-start.3
  220.1 0.6 copy-start.12
  250.0 3.8 copy-start.14
  253.7 5.7 %copy-start.13 = (f32[4,8]{0,1:T(8,128)S(1)}, f32[4,8]{0,1:T(8,128)}, u32[]{:S(2)}) copy-start(f32[4,8]{0,1:T(8,128)} %copy-done.12) | copy-start | bytes 388 | tf_op jit(solution)/shard_map/transpose(jvp())/while
  259.4 0.6 copy-start.12
  289.3 3.8 copy-start.14
  293.0 5.7 %copy-start.13 = (f32[4,8]{0,1:T(8,128)S(1)}, f32[4,8]{0,1:T(8,128)}, u32[]{:S(2)}) copy-start(f32[4,8]{0,1:T(8,128)} %copy-done.12) | copy-start | bytes 388 | tf_op jit(solution)/shard_map/transpose(jvp())/while
  298.7 0.6 copy-start.12
  328.6 3.8 copy-start.14
  332.4 5.7 %copy-start.13 = (f32[4,8]{0,1:T(8,128)S(1)}, f32[4,8]{0,1:T(8,128)}, u32[]{:S(2)}) copy-start(f32[4,8]{0,1:T(8,128)} %copy-done.12) | copy-start | bytes 388 | tf_op jit(solution)/shard_map/transpose(jvp())/while
  338.1 0.6 copy-start.12
  367.9 3.8 copy-start.14
  371.6 5.7 %copy-start.13 = (f32[4,8]{0,1:T(8,128)S(1)}, f32[4,8]{0,1:T(8,128)}, u32[]{:S(2)}) copy-start(f32[4,8]{0,1:T(8,128)} %copy-done.12) | copy-start | bytes 388 | tf_op jit(solution)/shard_map/transpose(jvp())/while
  377.4 58.3 %copy-start.2 = (f32[4,256,8,64]{1,3,2,0:T(8,128)S(1)}, f32[4,256,8,64]{1,3,2,0:T(8,128)}, u32[]{:S(2)}) copy-start(f32[4,256,8,64]{1,3,2,0:T(8,128)} %get-tuple-element.1033) | copy-start | bytes 6291460
  377.4 58.3 %copy-start.4 = (bf16[8,32,8,128]{3,2,0,1:T(8,128)(2,1)S(1)}, bf16[8,32,8,128]{3,2,0,1:T(8,128)(2,1)}, u32[]{:S(2)}) copy-start(bf16[8,32,8,128]{3,2,0,1:T(8,128)(2,1)} %copy-done.3) | copy-start | bytes 1572868
Sparse Core Ops, SparseCore 0:
  71.7 37.4 all-gather.4
